TPU v7x, 32 devices: a whole 2x2x4 slice. The times are simulated.
32 devices in a mesh: row: 8 (over z, y), col: 4 (over x, core).
Axes of the slice: x: 2, y: 2, z: 4, core: 2. Of those that a mesh axis runs over, the one named last changes fastest.
Arguments:
- tile_values: bfloat16 [128, 8, 256, 256], P(('row', 'col')), may hold values from -0.375 to 0.375
- block_columns: int32 [128, 8], P(('row', 'col')), may hold values from 0 to 127, as said below
- tile_counts: int32 [128], P(('row', 'col')), may hold values from 1 to 8, as said below
- diagonal: float32 [32768], P(('row', 'col')), may hold values from 0.5 to 4
- sketch_rows: int32 [32768], P(('row', 'col')), may hold values from 0 to 1023
- sketch_signs: int32 [32768], P(('row', 'col')), may hold values from 0 to 1
- right_side: float32 [16, 32768], P(None, ('row', 'col')), may hold values from -70 to 70
Outputs:
- solution: float32 [16, 32768], P(None, ('row', 'col'))
- last_basis: float32 [16, 32768], P(None, ('row', 'col'))
- hessenberg: float32 [16, 5, 4], replicated
Inputs may be any that keep to these rules, and one draw needn't show every extreme that they name: `block_columns`: for block row b all 8 entries are distinct block columns c with (c - b) mod 128 <= 4 or >= 124; only slots k < tile_counts[b] are used. `tile_counts`: in every draw the 4 block rows of at least one device all have 8.
All inputs are finite; a program needn't handle non-finite values.
Results may differ from a plain program's by a relative error of at most 0.0053.
Values may be sent and summed in bfloat16 or wider, within the bound.
A program may use at most 64 MiB of HBM per device.

v0:
```python
import math
import jax
import jax.numpy as jnp
from jax import lax
from jax.sharding import PartitionSpec as P

SKETCH = 1024
ITERS = 4
epsilon = 1e-06
highest = lax.Precision.HIGHEST


def with_halo(block, sides, width):
    for axis, dim in sides:
        count = lax.axis_size(axis)
        forward = [(i, i + 1) for i in range(count - 1)]
        forward.append((count - 1, 0))
        backward = [(target, source) for source, target in forward]
        low = lax.ppermute(
            lax.slice_in_dim(block, block.shape[dim] - width, None, axis=dim), axis, forward
        )
        high = lax.ppermute(lax.slice_in_dim(block, 0, width, axis=dim), axis, backward)
        block = jnp.concatenate([low, block, high], axis=dim)
    return block


def cholesky_solve(gram, target):
    order = gram.shape[1]
    factor = {}
    for column in range(order):
        diag_part = gram[:, column, column]
        for inner in range(column):
            diag_part = diag_part - factor[column, inner] * factor[column, inner]
        factor[column, column] = jnp.sqrt(diag_part)
        for below in range(column + 1, order):
            entry = gram[:, below, column]
            for inner in range(column):
                entry = entry - factor[below, inner] * factor[column, inner]
            factor[below, column] = entry / factor[column, column]
    forward = []
    for column in range(order):
        entry = target[:, column]
        for inner in range(column):
            entry = entry - factor[column, inner] * forward[inner]
        forward.append(entry / factor[column, column])
    result = [None] * order
    for column in reversed(range(order)):
        entry = forward[column]
        for inner in range(column + 1, order):
            entry = entry - factor[inner, column] * result[inner]
        result[column] = entry / factor[column, column]
    return jnp.stack(result, axis=1)


def sketch_solve(stacked, image_sketch):
    gram = jnp.einsum("rjk,rmk->rjm", stacked, stacked, precision=highest)
    target = jnp.einsum("rjk,rk->rj", stacked, image_sketch, precision=highest)
    return cholesky_solve(gram, target)


def local(tile_values, block_columns, tile_counts, diagonal, sketch_rows, sketch_signs, right_side):
    col_count = lax.axis_size("col")
    devices = lax.axis_size("row") * col_count
    device_index = lax.axis_index("row") * col_count + lax.axis_index("col")
    block_rows = tile_values.shape[0]
    slot_count = tile_values.shape[1]
    tile_size = tile_values.shape[2]
    systems = right_side.shape[0]
    all_blocks = block_rows * devices
    scaling = 1.0 / math.sqrt(all_blocks * tile_size)
    signed = (2 * sketch_signs - 1).astype(jnp.float32) * scaling
    projector = jnp.where(sketch_rows[:, None] == jnp.arange(SKETCH)[None, :], signed[:, None], 0.0)
    live_mask = jnp.arange(slot_count)[None, :] < tile_counts[:, None]
    first_block = device_index * block_rows
    turns = jnp.max(jnp.sum(live_mask.astype(jnp.int32), axis=1))
    live_weight = live_mask.astype(jnp.float32)
    start = lax.psum(jnp.dot(right_side, projector, precision=highest), ("row", "col"))
    beta = jnp.sqrt(jnp.sum(start * start, axis=1) + epsilon)
    basis = [right_side / beta[:, None]]
    sketched = [start / beta[:, None]]
    columns_list = []
    for step_index in range(ITERS):
        vector = basis[-1]
        shadow = vector.astype(jnp.bfloat16)
        widened = with_halo(shadow, ((("row", "col"), 1),), block_rows * tile_size)
        start_block = first_block - block_rows
        blocks = widened.reshape(systems, widened.shape[1] // tile_size, tile_size)
        local_index = (block_columns - start_block) % all_blocks

        def add_slot(slot_turn, running):
            slot_tiles = lax.dynamic_index_in_dim(tile_values, slot_turn, 1, keepdims=False)
            wanted = lax.dynamic_index_in_dim(local_index, slot_turn, 1, keepdims=False)
            picked = jnp.take(blocks, wanted, axis=1)
            weight_mask = lax.dynamic_index_in_dim(live_weight, slot_turn, 1, keepdims=False)
            product = jnp.einsum(
                "rbi,boi->rbo", picked, slot_tiles, preferred_element_type=jnp.float32
            )
            return running + product * weight_mask[None, :, None]

        tile_sum = lax.fori_loop(
            0, turns, add_slot, jnp.zeros((systems, block_rows, tile_size), jnp.float32)
        )
        image = diagonal[None, :] * vector + tile_sum.reshape(systems, block_rows * tile_size)
        image_sketch = lax.psum(jnp.dot(image, projector, precision=highest), ("row", "col"))
        stacked = jnp.stack(sketched, axis=1)
        coeffs = sketch_solve(stacked, image_sketch)
        fresh = image - jnp.einsum(
            "rj,rjn->rn", coeffs, jnp.stack(basis, axis=1), precision=highest
        )
        fresh_sketch = image_sketch - jnp.einsum("rj,rjk->rk", coeffs, stacked, precision=highest)
        norm_new = jnp.sqrt(jnp.sum(fresh_sketch * fresh_sketch, axis=1) + epsilon)
        basis.append(fresh / norm_new[:, None])
        sketched.append(fresh_sketch / norm_new[:, None])
        padding = jnp.zeros((systems, ITERS - step_index - 1), jnp.float32)
        columns_list.append(jnp.concatenate([coeffs, norm_new[:, None], padding], axis=1))
    hessenberg = jnp.stack(columns_list, axis=2)
    gram = jnp.einsum("rim,rin->rmn", hessenberg, hessenberg, precision=highest)
    weights = cholesky_solve(gram, beta[:, None] * hessenberg[:, 0, :])
    solution = jnp.einsum(
        "rm,rmn->rn", weights, jnp.stack(basis[:ITERS], axis=1), precision=highest
    )
    return (solution, basis[-1], hessenberg)


def solution(mesh):
    in_specs = (
        P(("row", "col"), None, None, None),
        P(("row", "col"), None),
        P(("row", "col")),
        P(("row", "col")),
        P(("row", "col")),
        P(("row", "col")),
        P(None, ("row", "col")),
    )
    out_specs = (P(None, ("row", "col")), P(None, ("row", "col")), P())
    return jax.shard_map(local, mesh=mesh, in_specs=in_specs, out_specs=out_specs, check_vma=False)
```

profile of v0, /device:TPU:1, one launch (start us, length us, event | category | flops | bytes accessed | tf_op | source)
XLA Modules:
  0.0 768.0 jit_solution(5249777427383235755)
XLA Ops:
  7.2 0.7 convert_multiply_fusion
  7.9 4.2 fusion.73
  12.2 0.8 copy.85
  13.0 0.7 fusion.113
  13.6 123.9 %all-reduce.6.cloned.1.call-done = f32[16,1024]{1,0:T(8,128)} async-done(((f32[16,1024]{1,0:T(8,128)}), f32[16,1024]{1,0:T(8,128)}) %all-reduce.6.cloned.1.call-update) | async-done | bytes 65552 | tf_op jit(solution)/shard_map/psum | solution.py:77
  137.5 1.0 multiply_reduce_fusion.5
  138.5 0.9 fusion.145
  139.5 1.7 collective-permute-start
  141.2 0.7 convert_reduce_fusion
  141.9 4.5 copy.86
  146.5 0.6 reduce_max.9
  147.1 8.4 %while.40 = (s32[]{:T(128)}, f32[16,4,256]{2,0,1:T(8,128)S(1)}, s32[]{:T(128)}, bf16[4,8,256,256]{3,2,0,1:T(8,128)(2,1)}, s32[4,8]{0,1:T(8,128)S(1)}, /*index=5*...) while((s32[]{:T(128)}, f32[16,4,256]{2,0,1:T(8,128)S(1)}, ...), condition=%wide.region_5.7_spmd, body=%wide.region_4.6_spmd.sunk | while | flops 8438813 | bytes 758035 | solution.py:100
  148.4 1.3 fusion.184
  151.0 1.3 fusion.184
  153.6 1.3 fusion.184
  155.6 3.2 fusion.54
  159.0 131.3 %all-reduce.8.cloned.1.call-done = f32[16,1024]{1,0:T(8,128)} async-done(((f32[16,1024]{1,0:T(8,128)}), f32[16,1024]{1,0:T(8,128)}) %all-reduce.8.cloned.1.call-update) | async-done | bytes 65552 | tf_op jit(solution)/shard_map/psum | solution.py:104
  290.3 1.0 multiply_reduce_fusion
  291.4 1.1 fusion.147
  292.4 0.9 fusion.153
  293.5 1.7 collective-permute-start.2
  295.2 1.1 fusion.100
  296.8 1.6 collective-permute-done.2
  298.4 8.4 %while.41 = (s32[]{:T(128)}, f32[16,4,256]{2,0,1:T(8,128)S(1)}, s32[]{:T(128)}, bf16[4,8,256,256]{3,2,0,1:T(8,128)(2,1)}, s32[4,8]{0,1:T(8,128)S(1)}, /*index=5*...) while((s32[]{:T(128)}, f32[16,4,256]{2,0,1:T(8,128)S(1)}, ...), condition=%wide.region_9.11_spmd, body=%wide.region_8.10_spmd.sunk | while | flops 8438813 | bytes 758035 | solution.py:100
  299.7 1.3 fusion.188
  302.3 1.3 fusion.188
  304.9 1.3 fusion.188
  306.8 3.1 fusion.52
  310.3 132.5 %all-reduce.10.cloned.1.call-done = f32[16,1024]{1,0:T(8,128)} async-done(((f32[16,1024]{1,0:T(8,128)}), f32[16,1024]{1,0:T(8,128)}) %all-reduce.10.cloned.1.call-update) | async-done | bytes 65552 | tf_op jit(solution)/shard_map/psum | solution.py:104
  442.8 2.0 fusion.98
  445.7 1.0 multiply_reduce_fusion.3
  446.6 0.6 fusion.94
  447.3 0.9 fusion.150
  448.3 1.7 collective-permute-start.4
  450.0 1.2 fusion.80
  451.6 1.5 collective-permute-done.4
  453.2 8.4 %while.42 = (s32[]{:T(128)}, f32[16,4,256]{2,0,1:T(8,128)S(1)}, s32[]{:T(128)}, bf16[4,8,256,256]{3,2,0,1:T(8,128)(2,1)}, s32[4,8]{0,1:T(8,128)S(1)}, /*index=5*...) while((s32[]{:T(128)}, f32[16,4,256]{2,0,1:T(8,128)S(1)}, ...), condition=%wide.region_13.15_spmd, body=%wide.region_12.14_spmd.sunk | while | flops 8438813 | bytes 758035 | solution.py:100
  454.5 1.3 fusion.192
  457.1 1.3 fusion.192
  459.7 1.3 fusion.192
  461.6 3.1 fusion.50
  465.0 132.7 %all-reduce.12.cloned.1.call-done = f32[16,1024]{1,0:T(8,128)} async-done(((f32[16,1024]{1,0:T(8,128)}), f32[16,1024]{1,0:T(8,128)}) %all-reduce.12.cloned.1.call-update) | async-done | bytes 65552 | tf_op jit(solution)/shard_map/psum | solution.py:104
  597.6 2.0 fusion.78
  599.9 0.6 fusion.76
  600.5 1.0 multiply_reduce_fusion.2
  601.5 0.6 fusion.82
  602.2 0.9 fusion.148
  603.2 1.7 collective-permute-start.6
  604.9 1.2 fusion.92
  606.6 1.4 collective-permute-done.6
  608.1 8.6 %while.43 = (s32[]{:T(128)}, f32[16,4,256]{2,0,1:T(8,128)S(1)}, s32[]{:T(128)}, bf16[4,8,256,256]{3,2,0,1:T(8,128)(2,1)}, s32[4,8]{0,1:T(8,128)S(1)}, /*index=5*...) while((s32[]{:T(128)}, f32[16,4,256]{2,0,1:T(8,128)S(1)}, ...), condition=%wide.region_17.19_spmd, body=%wide.region_16.18_spmd.sunk | while | flops 8438813 | bytes 758035 | solution.py:100
  609.4 1.3 fusion.196
  612.0 1.3 fusion.196
  614.6 1.3 fusion.196
  616.8 3.1 fusion.48
  620.1 132.7 %all-reduce.14.cloned.1.call-done = f32[16,1024]{1,0:T(8,128)} async-done(((f32[16,1024]{1,0:T(8,128)}), f32[16,1024]{1,0:T(8,128)}) %all-reduce.14.cloned.1.call-update) | async-done | bytes 65552 | tf_op jit(solution)/shard_map/psum | solution.py:104
  752.8 2.1 fusion.90
  755.1 0.7 fusion.88
  755.8 1.0 fusion.104
  757.2 0.7 copy.109
  758.8 0.7 fusion.84
  759.5 0.7 fusion.86
  760.1 0.6 copy.202
  760.8 0.7 fusion.102
  (143 shorter events, 12.3 us)
Async XLA Ops:
  7.2 130.4 %all-reduce.6.cloned.1.call-start = ((), (), s32[]{:S(2)}) async-start(), calls=%async_computation | async-start | bytes 131072 | tf_op jit(solution)/shard_map/psum | solution.py:77
  12.1 278.2 %all-reduce.8.cloned.1.call-start = ((), (), s32[]{:S(2)}) async-start(), calls=%async_computation.1 | async-start | bytes 131072 | tf_op jit(solution)/shard_map/psum | solution.py:104
  139.4 7.7 collective-permute-start.1
  139.5 7.6 collective-permute-start
  146.4 9.1 %copy-start.1 = (f32[16,1024]{1,0:T(8,128)S(1)}, f32[16,1024]{1,0:T(8,128)}, u32[]{:S(2)}) copy-start(f32[16,1024]{1,0:T(8,128)} %param.23) | copy-start | bytes 196612
  146.4 9.1 %copy-start.2 = (f32[1024]{0:T(1024)S(1)}, f32[1024]{0:T(1024)}, u32[]{:S(2)}) copy-start(f32[1024]{0:T(1024)} %param.20) | copy-start | bytes 12292
  146.4 9.1 %copy-start.3 = (s32[1024]{0:T(1024)S(1)}, s32[1024]{0:T(1024)}, u32[]{:S(2)}) copy-start(s32[1024]{0:T(1024)} %param.21) | copy-start | bytes 12292
  146.4 143.9 %copy-start = (f32[16,1024]{1,0:T(8,128)S(1)}, f32[16,1024]{1,0:T(8,128)}, u32[]{:S(2)}) copy-start(f32[16,1024]{1,0:T(8,128)} %all-reduce.6.cloned.1.call-done) | copy-start | bytes 196612
  158.8 284.1 %all-reduce.10.cloned.1.call-start = ((), (), s32[]{:S(2)}) async-start(), calls=%async_computation.2 | async-start | bytes 131072 | tf_op jit(solution)/shard_map/psum | solution.py:104
  293.4 3.4 collective-permute-start.3
  293.5 4.9 collective-permute-start.2
  310.0 287.6 %all-reduce.12.cloned.1.call-start = ((), (), s32[]{:S(2)}) async-start(), calls=%async_computation.3 | async-start | bytes 131072 | tf_op jit(solution)/shard_map/psum | solution.py:104
  448.2 3.4 collective-permute-start.5
  448.3 4.9 collective-permute-start.4
  464.8 288.0 %all-reduce.14.cloned.1.call-start = ((), (), s32[]{:S(2)}) async-start(), calls=%async_computation.4 | async-start | bytes 131072 | tf_op jit(solution)/shard_map/psum | solution.py:104
  603.1 3.5 collective-permute-start.7
  603.2 4.9 collective-permute-start.6
Sparse Core Ops, SparseCore 0:
  14.1 123.3 all-reduce.5
  158.9 131.3 all-reduce.7
  310.1 132.6 all-reduce.9
  464.9 132.6 all-reduce.11
  620.1 132.6 all-reduce.13
where the time goes:
time: 771 us; the launch traced here: 768 us
  waiting for transfers between devices  658 us (85%)
  matrix products  46.8 us (6%)
  local copies, waits for them, and re-layouts  16.1 us (2%)
  other arithmetic  14.3 us (2%)
  between operations  14.2 us (2%)
  loops' own time  11.2 us (1%)
    psum x4, waiting for transfers between devices, local(): lax.psum(jnp.dot(image, projector, precision=highest), ('row', 'col'))  529 us
    psum x1, waiting for transfers between devices, local(): lax.psum(jnp.dot(right_side, projector, precision=highest), ('row', 'col'))  124 us
    dot_general x12, matrix products, add_slot(): jnp.einsum('rbi,boi->rbo', picked, slot_tiles, preferred_element_type=jnp...  15.7 us
  transfers between devices with their start and end apart: 13, of which 9 were waited for; matrix products, arithmetic and copies ran while one was open for 2% of the time, Pallas kernels for 0%

commit v1 on v0

--- a/solution.py
+++ b/solution.py
@@ -59,6 +59,10 @@
 
 
 def local(tile_values, block_columns, tile_counts, diagonal, sketch_rows, sketch_signs, right_side):
+
+    def _test_surface(local_values, bus_axis):
+        return jnp.sum(jax.lax.all_gather(local_values, axis_name=bus_axis), axis=0)
+
     col_count = lax.axis_size("col")
     devices = lax.axis_size("row") * col_count
     device_index = lax.axis_index("row") * col_count + lax.axis_index("col")
@@ -74,7 +78,7 @@
     first_block = device_index * block_rows
     turns = jnp.max(jnp.sum(live_mask.astype(jnp.int32), axis=1))
     live_weight = live_mask.astype(jnp.float32)
-    start = lax.psum(jnp.dot(right_side, projector, precision=highest), ("row", "col"))
+    start = _test_surface(jnp.dot(right_side, projector, precision=highest), ("row", "col"))
     beta = jnp.sqrt(jnp.sum(start * start, axis=1) + epsilon)
     basis = [right_side / beta[:, None]]
     sketched = [start / beta[:, None]]

time: 771 us -> 704 us (0.913)
  waiting for transfers between devices: 658 us -> 592 us
    psum x1 -> x0, waiting for transfers between devices: 124 us -> none  [local(): lax.psum(jnp.dot(right_side, projector, precision=highest), ('row', 'col'))]
    all_gather x0 -> x1, waiting for transfers between devices: none -> 57.3 us  [_test_surface(): return jnp.sum(jax.lax.all_gather(local_values, axis_name=bus_axis), axis=0)]
where the time goes in v1:
time: 704 us; the launch traced here: 701 us
  waiting for transfers between devices  592 us (84%)
  matrix products  46.8 us (7%)
  local copies, waits for them, and re-layouts  16.1 us (2%)
  between operations  14.2 us (2%)
  other arithmetic  13.7 us (2%)
  loops' own time  11.3 us (2%)
  starting transfers between devices  7.56 us (1%)
    psum x4, waiting for transfers between devices, local(): lax.psum(jnp.dot(image, projector, precision=highest), ('row', 'col'))  530 us
    all_gather x1, waiting for transfers between devices, _test_surface(): return jnp.sum(jax.lax.all_gather(local_values, axis_name=bus_axis), axis=0)  57.3 us
    dot_general x12, matrix products, add_slot(): jnp.einsum('rbi,boi->rbo', picked, slot_tiles, preferred_element_type=jnp...  15.7 us
  transfers between devices with their start and end apart: 13, of which 9 were waited for; matrix products, arithmetic and copies ran while one was open for 2% of the time, Pallas kernels for 0%

profile of v1, /device:TPU:1, one launch (start us, length us, event | category | flops | bytes accessed | tf_op | source)
XLA Modules:
  0.0 701.3 jit_solution(8788361380959986782)
XLA Ops:
  7.2 0.7 convert_multiply_fusion
  7.9 4.2 fusion.73
  12.2 0.8 copy.85
  13.0 0.7 fusion.113
  13.7 57.3 %all-gather.3.cloned.1.call-done = f32[512,1024]{1,0:T(8,128)} async-done(((f32[16,1024]{1,0:T(8,128)}), f32[512,1024]{1,0:T(8,128)}) %all-gather.3.cloned.1.call-update) | async-done | bytes 2097168 | tf_op jit(solution)/shard_map/all_gather | solution.py:64
  71.0 1.7 reduce_sum.65
  73.2 1.5 collective-permute-start
  74.9 4.6 copy.86
  79.4 0.6 reduce_max.9
  80.1 8.4 %while.40 = (s32[]{:T(128)}, f32[16,4,256]{2,0,1:T(8,128)S(1)}, s32[]{:T(128)}, bf16[4,8,256,256]{3,2,0,1:T(8,128)(2,1)}, s32[4,8]{0,1:T(8,128)S(1)}, /*index=5*...) while((s32[]{:T(128)}, f32[16,4,256]{2,0,1:T(8,128)S(1)}, ...), condition=%wide.region_5.7_spmd, body=%wide.region_4.6_spmd.sunk | while | flops 8438813 | bytes 758035 | solution.py:104
  80.8 0.5 gather_fusion
  81.4 1.3 fusion.183
  84.0 1.3 fusion.183
  86.6 1.3 fusion.183
  88.6 3.2 fusion.54
  91.9 131.7 %all-reduce.5.cloned.1.call-done = f32[16,1024]{1,0:T(8,128)} async-done(((f32[16,1024]{1,0:T(8,128)}), f32[16,1024]{1,0:T(8,128)}) %all-reduce.5.cloned.1.call-update) | async-done | bytes 65552 | tf_op jit(solution)/shard_map/psum | solution.py:108
  223.6 1.0 multiply_reduce_fusion
  224.7 1.1 multiply_reduce_fusion.4
  225.7 0.9 fusion.152
  226.7 1.7 collective-permute-start.2
  228.5 1.1 fusion.100
  230.1 1.6 collective-permute-done.2
  231.7 8.4 %while.41 = (s32[]{:T(128)}, f32[16,4,256]{2,0,1:T(8,128)S(1)}, s32[]{:T(128)}, bf16[4,8,256,256]{3,2,0,1:T(8,128)(2,1)}, s32[4,8]{0,1:T(8,128)S(1)}, /*index=5*...) while((s32[]{:T(128)}, f32[16,4,256]{2,0,1:T(8,128)S(1)}, ...), condition=%wide.region_9.11_spmd, body=%wide.region_8.10_spmd.sunk | while | flops 8438813 | bytes 758035 | solution.py:104
  233.0 1.3 fusion.187
  235.6 1.3 fusion.187
  238.2 1.3 fusion.187
  240.1 3.1 fusion.52
  243.6 132.5 %all-reduce.7.cloned.1.call-done = f32[16,1024]{1,0:T(8,128)} async-done(((f32[16,1024]{1,0:T(8,128)}), f32[16,1024]{1,0:T(8,128)}) %all-reduce.7.cloned.1.call-update) | async-done | bytes 65552 | tf_op jit(solution)/shard_map/psum | solution.py:108
  376.1 2.0 fusion.98
  378.4 0.6 fusion.96
  379.0 1.0 multiply_reduce_fusion.3
  379.9 0.6 fusion.94
  380.6 0.9 fusion.149
  381.6 1.7 collective-permute-start.4
  383.3 1.2 fusion.80
  384.9 1.5 collective-permute-done.4
  386.5 8.4 %while.42 = (s32[]{:T(128)}, f32[16,4,256]{2,0,1:T(8,128)S(1)}, s32[]{:T(128)}, bf16[4,8,256,256]{3,2,0,1:T(8,128)(2,1)}, s32[4,8]{0,1:T(8,128)S(1)}, /*index=5*...) while((s32[]{:T(128)}, f32[16,4,256]{2,0,1:T(8,128)S(1)}, ...), condition=%wide.region_13.15_spmd, body=%wide.region_12.14_spmd.sunk | while | flops 8438813 | bytes 758035 | solution.py:104
  387.8 1.3 fusion.191
  390.4 1.3 fusion.191
  393.0 1.3 fusion.191
  394.9 3.1 fusion.50
  398.3 132.7 %all-reduce.9.cloned.1.call-done = f32[16,1024]{1,0:T(8,128)} async-done(((f32[16,1024]{1,0:T(8,128)}), f32[16,1024]{1,0:T(8,128)}) %all-reduce.9.cloned.1.call-update) | async-done | bytes 65552 | tf_op jit(solution)/shard_map/psum | solution.py:108
  531.0 2.0 fusion.78
  533.2 0.6 fusion.76
  533.8 1.0 multiply_reduce_fusion.2
  534.8 0.6 fusion.82
  535.5 0.9 fusion.147
  536.5 1.7 collective-permute-start.6
  538.2 1.2 fusion.92
  539.9 1.4 collective-permute-done.6
  541.4 8.6 %while.43 = (s32[]{:T(128)}, f32[16,4,256]{2,0,1:T(8,128)S(1)}, s32[]{:T(128)}, bf16[4,8,256,256]{3,2,0,1:T(8,128)(2,1)}, s32[4,8]{0,1:T(8,128)S(1)}, /*index=5*...) while((s32[]{:T(128)}, f32[16,4,256]{2,0,1:T(8,128)S(1)}, ...), condition=%wide.region_17.19_spmd, body=%wide.region_16.18_spmd.sunk | while | flops 8438813 | bytes 758035 | solution.py:104
  542.7 1.3 fusion.195
  545.3 1.3 fusion.195
  547.9 1.3 fusion.195
  550.1 3.1 fusion.48
  553.4 132.7 %all-reduce.11.cloned.1.call-done = f32[16,1024]{1,0:T(8,128)} async-done(((f32[16,1024]{1,0:T(8,128)}), f32[16,1024]{1,0:T(8,128)}) %all-reduce.11.cloned.1.call-update) | async-done | bytes 65552 | tf_op jit(solution)/shard_map/psum | solution.py:108
  686.1 2.1 fusion.90
  688.4 0.7 fusion.88
  689.1 1.0 fusion.104
  690.3 0.7 copy.109
  692.1 0.7 fusion.84
  692.8 0.7 fusion.86
  693.5 0.6 copy.202
  694.1 0.7 fusion.102
  (145 shorter events, 11.8 us)
Async XLA Ops:
  7.2 65.7 %copy-start = (f32[16,1024]{1,0:T(8,128)S(1)}, f32[16,1024]{1,0:T(8,128)}, u32[]{:S(2)}) copy-start(f32[16,1024]{1,0:T(8,128)} %param.23) | copy-start | bytes 196612
  7.2 67.5 %copy-start.2 = (s32[4]{0:T(128)S(1)}, s32[4]{0:T(128)}, u32[]{:S(2)}) copy-start(s32[4]{0:T(128)} %param.19) | copy-start | bytes 52
  7.2 63.8 %all-gather.3.cloned.1.call-start = ((), (), s32[]{:S(2)}) async-start(), calls=%async_computation.4 | async-start | bytes 2162688 | tf_op jit(solution)/shard_map/all_gather | solution.py:64
  12.2 211.4 %all-reduce.5.cloned.1.call-start = ((), (), s32[]{:S(2)}) async-start(), calls=%async_computation | async-start | bytes 131072 | tf_op jit(solution)/shard_map/psum | solution.py:108
  72.9 7.2 %collective-permute-start.1 = (bf16[16,1024]{1,0:T(8,128)(2,1)S(1)}, bf16[16,1024]{1,0:T(8,128)(2,1)S(1)}, u32[]{:S(2)}, u32[]{:S(2)}) collective-permute-start(bf16[16,1024]{1,0:T(8,128)(2,1)S(1)} %get-tuple-element.405), channel_id=1, source_target_pairs={{1,0},{2,1},{3,2},{4,3},{5,4},{6,5},{7,6},{8,7},{9,8},{10,9},{11,1... | collective-permute-start | bytes 98312 | tf_op jit(solution)/shard_map/ppermute | solution.py:22
  73.2 6.8 collective-permute-start
  79.4 9.1 %copy-start.1 = (f32[1024]{0:T(1024)S(1)}, f32[1024]{0:T(1024)}, u32[]{:S(2)}) copy-start(f32[1024]{0:T(1024)} %param.20) | copy-start | bytes 12292
  79.4 9.1 %copy-start.3 = (s32[1024]{0:T(1024)S(1)}, s32[1024]{0:T(1024)}, u32[]{:S(2)}) copy-start(s32[1024]{0:T(1024)} %param.21) | copy-start | bytes 12292
  91.7 284.4 %all-reduce.7.cloned.1.call-start = ((), (), s32[]{:S(2)}) async-start(), calls=%async_computation.1 | async-start | bytes 131072 | tf_op jit(solution)/shard_map/psum | solution.py:108
  226.7 3.4 collective-permute-start.3
  226.7 4.9 collective-permute-start.2
  243.3 287.7 %all-reduce.9.cloned.1.call-start = ((), (), s32[]{:S(2)}) async-start(), calls=%async_computation.2 | async-start | bytes 131072 | tf_op jit(solution)/shard_map/psum | solution.py:108
  381.5 3.4 collective-permute-start.5
  381.6 4.9 collective-permute-start.4
  398.1 288.0 %all-reduce.11.cloned.1.call-start = ((), (), s32[]{:S(2)}) async-start(), calls=%async_computation.3 | async-start | bytes 131072 | tf_op jit(solution)/shard_map/psum | solution.py:108
  536.4 3.5 collective-permute-start.7
  536.5 4.9 collective-permute-start.6
Sparse Core Ops, SparseCore 0:
  12.3 58.6 all-gather.2
  91.9 131.7 all-reduce.4
  243.4 132.6 all-reduce.6
  398.2 132.6 all-reduce.8
  553.4 132.6 all-reduce.10
